TPU v7x, 32 devices: a whole 2x2x4 slice. The times are simulated.
32 devices in a mesh: dp: 16 (over z, y, x), seq: 2 (over core).
Axes of the slice: x: 2, y: 2, z: 4, core: 2. Of those that a mesh axis runs over, the one named last changes fastest.
Arguments:
- chains_in: bfloat16 [128, 160, 768], P(('dp', 'seq')), may hold values from -6 to 6
- lengths: int32 [128], P(('dp', 'seq')), may hold values from 95 to 160
- d_out: bfloat16 [128, 160, 768], P(('dp', 'seq')), may hold values from -6 to 6
- w_query: bfloat16 [768, 768], replicated, may hold values from -0.21875 to 0.21875
- b_query: float32 [768], replicated, may hold values from -3 to 3
- w_key: bfloat16 [768, 768], replicated, may hold values from -0.21875 to 0.21875
- w_value: bfloat16 [768, 768], replicated, may hold values from -0.21875 to 0.21875
- b_value: float32 [768], replicated, may hold values from -3 to 3
- w_output: bfloat16 [768, 768], replicated, may hold values from -2.5 to 2.5
- b_output: float32 [768], replicated, may hold values from -3 to 3
- gain_one: float32 [768], replicated, may hold values from 0.25 to 1.75
- shift_one: float32 [768], replicated, may hold values from -2 to 2
- w_inner: bfloat16 [768, 3072], replicated, may hold values from -0.21875 to 0.21875
- b_inner: float32 [3072], replicated, may hold values from -3 to 3
- w_outer: bfloat16 [3072, 768], replicated, may hold values from -0.109375 to 0.109375
- b_outer: float32 [768], replicated, may hold values from -3 to 3
- gain_two: float32 [768], replicated, may hold values from 0.25 to 1.75
- shift_two: float32 [768], replicated, may hold values from -2 to 2
Outputs:
- layer_out: bfloat16 [128, 160, 768], P(('dp', 'seq'))
- d_x: float32 [128, 160, 768], P(('dp', 'seq'))
- d_w_query: float32 [768, 768], replicated
- d_b_query: float32 [768], replicated
- d_w_key: float32 [768, 768], replicated
- d_w_value: float32 [768, 768], replicated
- d_b_value: float32 [768], replicated
- d_w_output: float32 [768, 768], replicated
- d_b_output: float32 [768], replicated
- d_gain_one: float32 [768], replicated
- d_shift_one: float32 [768], replicated
- d_w_inner: float32 [768, 3072], replicated
- d_b_inner: float32 [3072], replicated
- d_w_outer: float32 [3072, 768], replicated
- d_b_outer: float32 [768], replicated
- d_gain_two: float32 [768], replicated
- d_shift_two: float32 [768], replicated
Inputs may be any that keep to these rules, and one draw needn't show every extreme that they name: `lengths`: every chain fills more than half of its 160 positions.
All inputs are finite; a program needn't handle non-finite values.
Results may differ from a plain program's by a relative error of at most 0.015.
Values may be sent and summed in bfloat16 or wider, within the bound.
No kernel may reach another device: no remote copies, remote signals or barrier semaphores. Data moves between devices by JAX's collectives and lax.ppermute only.
A program may use at most 256 MiB of HBM per device.

v0:
```python
import jax
import jax.numpy as jnp
from jax import lax
from jax.sharding import PartitionSpec as P

H = 12
EPS = 1e-12


def norm_forward(h, gain, shift):
    centre = h - jnp.mean(h, -1, keepdims=True)
    scale = lax.rsqrt(jnp.mean(centre * centre, -1, keepdims=True) + EPS)
    unit = centre * scale
    return (unit * gain + shift, unit, scale)


def norm_backward(grad, unit, scale, gain):
    d_gain = jnp.sum(grad * unit, 0)
    d_shift = jnp.sum(grad, 0)
    inner = grad * gain
    d_h = scale * (
        inner
        - jnp.mean(inner, -1, keepdims=True)
        - unit * jnp.mean(inner * unit, -1, keepdims=True)
    )
    return (d_h, d_gain, d_shift)


def over_rows(left, right):
    return lax.dot_general(
        left, right, (((0,), (0,)), ((), ())), preferred_element_type=jnp.float32
    )


def times_trans(left, weight):
    return lax.dot_general(
        left, weight, (((1,), (1,)), ((), ())), preferred_element_type=jnp.float32
    )


def attn_scores(query, keys, live_keys):
    seqs, count, width = query.shape
    total = keys.shape[1]
    size = width // H
    q_heads = query.reshape(seqs, count, H, size)
    k_heads = keys.reshape(seqs, total, H, size)
    scores = (
        jnp.einsum("bqhe,bkhe->bhqk", q_heads, k_heads, preferred_element_type=jnp.float32) * 0.125
    )
    return jnp.where(live_keys[:, None, None, :], scores, -1000000000.0)


def packed(grads, count):
    flat = jnp.concatenate([g.reshape(-1) for g in grads])
    extra = -flat.shape[0] % count
    return flat.reshape(count, -1)


def unpacked(flat, grads):
    flat = flat.reshape(-1)
    pieces = []
    start = 0
    for grad in grads:
        number = grad.size
        pieces.append(flat[start : start + number].reshape(grad.shape))
        start = start + number
    return tuple(pieces)


def body(
    chains_in,
    lengths,
    d_out,
    w_query,
    b_query,
    w_key,
    w_value,
    b_value,
    w_output,
    b_output,
    gain_one,
    shift_one,
    w_inner,
    b_inner,
    w_outer,
    b_outer,
    gain_two,
    shift_two,
):
    f32 = jnp.float32
    low_type = jnp.bfloat16
    seqs, length, width = chains_in.shape
    rows = seqs * length
    size = width // H
    parts = lax.axis_size("dp")
    count = lax.axis_size("dp") * lax.axis_size("seq")
    place = jnp.arange(length, dtype=jnp.int32)
    live_rows = place[None, :] < lengths[:, None]
    flat_x = chains_in.reshape(rows, width)
    query = (
        (jnp.dot(flat_x, w_query, preferred_element_type=f32) + b_query)
        .astype(low_type)
        .reshape(seqs, length, width)
    )
    keys = (
        jnp.dot(flat_x, w_key, preferred_element_type=f32)
        .astype(low_type)
        .reshape(seqs, length, width)
    )
    values = (
        (jnp.dot(flat_x, w_value, preferred_element_type=f32) + b_value)
        .astype(low_type)
        .reshape(seqs, length, width)
    )
    scores = attn_scores(query, keys, live_rows)
    top = jnp.max(scores, -1, keepdims=True)
    expo = jnp.exp(scores - top)
    summed = jnp.sum(expo, -1, keepdims=True)
    prob_b = (expo / summed).astype(low_type)
    lse = top + jnp.log(summed)
    v_heads = values.reshape(seqs, length, H, size)
    mixed = (
        jnp.einsum("bhqk,bkhe->bqhe", prob_b, v_heads, preferred_element_type=f32)
        .reshape(rows, width)
        .astype(low_type)
    )
    h_one = flat_x.astype(f32) + jnp.dot(mixed, w_output, preferred_element_type=f32) + b_output
    first, unit_one, scale_one = norm_forward(h_one, gain_one, shift_one)
    live_flat = live_rows.reshape(rows)
    fin = first.astype(low_type)
    pre = jnp.dot(fin, w_inner, preferred_element_type=f32) + b_inner
    hidden = jax.nn.gelu(pre, approximate=False).astype(low_type)
    ffn_home = (jnp.dot(hidden, w_outer, preferred_element_type=f32) + b_outer).astype(low_type)
    h_two = first + ffn_home.astype(f32)
    second, unit_two, scale_two = norm_forward(h_two, gain_two, shift_two)
    keep = live_flat[:, None].astype(f32)
    layer_out = (second * keep).astype(low_type).reshape(seqs, length, width)
    grad_out = d_out.reshape(rows, width).astype(f32) * keep
    d_h_two, d_gain_two, d_shift_two = norm_backward(grad_out, unit_two, scale_two, gain_two)
    d_ffn = d_h_two.astype(low_type)
    d_w_outer = over_rows(hidden, d_ffn)
    d_b_outer = jnp.sum(d_ffn.astype(f32), 0)
    d_hidden = times_trans(d_ffn, w_outer)
    gelu_pull = jax.vjp(lambda z: jax.nn.gelu(z, approximate=False), pre)[1]
    d_pre = gelu_pull(d_hidden)[0].astype(low_type)
    d_w_inner = over_rows(fin, d_pre)
    d_b_inner = jnp.sum(d_pre.astype(f32), 0)
    d_fin = times_trans(d_pre, w_inner).astype(low_type)
    d_home = d_fin
    d_first = d_h_two + d_home.astype(f32)
    ffn_grads = (d_w_inner, d_b_inner, d_w_outer, d_b_outer, d_gain_two, d_shift_two)
    d_h_one, d_gain_one, d_shift_one = norm_backward(d_first, unit_one, scale_one, gain_one)
    d_attn = d_h_one.astype(low_type)
    d_w_output = over_rows(mixed, d_attn)
    d_b_output = jnp.sum(d_attn.astype(f32), 0)
    d_mixed = times_trans(d_attn, w_output).astype(low_type).reshape(seqs, length, H, size)
    scores = attn_scores(query, keys, live_rows)
    prob = jnp.exp(scores - lse)
    prob_b = prob.astype(low_type)
    d_prob = jnp.einsum("bqhe,bkhe->bhqk", d_mixed, v_heads, preferred_element_type=f32)
    delta = jnp.sum(prob * d_prob, -1, keepdims=True)
    d_scores = (prob * (d_prob - delta)).astype(low_type)
    k_heads = keys.reshape(seqs, length, H, size)
    q_heads = query.reshape(seqs, length, H, size)
    d_query = (
        (jnp.einsum("bhqk,bkhe->bqhe", d_scores, k_heads, preferred_element_type=f32) * 0.125)
        .astype(low_type)
        .reshape(rows, width)
    )
    d_key = (
        (jnp.einsum("bhqk,bqhe->bkhe", d_scores, q_heads, preferred_element_type=f32) * 0.125)
        .astype(low_type)
        .reshape(rows, width)
    )
    d_value = (
        jnp.einsum("bhqk,bqhe->bkhe", prob_b, d_mixed, preferred_element_type=f32)
        .astype(low_type)
        .reshape(rows, width)
    )
    d_w_query = over_rows(flat_x, d_query)
    d_b_query = jnp.sum(d_query.astype(f32), 0)
    d_w_key = over_rows(flat_x, d_key)
    d_w_value = over_rows(flat_x, d_value)
    d_b_value = jnp.sum(d_value.astype(f32), 0)
    d_x = (
        d_h_one
        + times_trans(d_query, w_query)
        + times_trans(d_key, w_key)
        + times_trans(d_value, w_value)
    )
    d_x = d_x.reshape(seqs, length, width)
    attn_grads = (
        d_w_query,
        d_b_query,
        d_w_key,
        d_w_value,
        d_b_value,
        d_w_output,
        d_b_output,
        d_gain_one,
        d_shift_one,
    )
    local_grads = attn_grads + ffn_grads
    big = [g for g in local_grads if g.ndim == 2]
    small = [g for g in local_grads if g.ndim == 1]
    sums = lax.psum(jnp.concatenate(small), ("dp", "seq"))
    small_sums = unpacked(sums, small)
    big_sums = []
    for grad in big:
        part = lax.psum_scatter(
            grad.astype(low_type), ("dp", "seq"), scatter_dimension=0, tiled=True
        )
        big_sums.append(lax.all_gather(part, ("dp", "seq"), axis=0, tiled=True).astype(f32))
    every = []
    for grad in local_grads:
        every.append(big_sums.pop(0) if grad.ndim == 2 else small_sums[0])
        small_sums = small_sums if grad.ndim == 2 else small_sums[1:]
    return (
        layer_out,
        d_x,
        every[0],
        every[1],
        every[2],
        every[3],
        every[4],
        every[5],
        every[6],
        every[7],
        every[8],
        every[9],
        every[10],
        every[11],
        every[12],
        every[13],
        every[14],
    )


def solution(mesh):
    return jax.shard_map(
        body,
        mesh=mesh,
        in_specs=(
            P(("dp", "seq"), None, None),
            P(("dp", "seq")),
            P(("dp", "seq"), None, None),
            P(),
            P(),
            P(),
            P(),
            P(),
            P(),
            P(),
            P(),
            P(),
            P(),
            P(),
            P(),
            P(),
            P(),
            P(),
        ),
        out_specs=(
            P(("dp", "seq"), None, None),
            P(("dp", "seq"), None, None),
            P(),
            P(),
            P(),
            P(),
            P(),
            P(),
            P(),
            P(),
            P(),
            P(),
            P(),
            P(),
            P(),
            P(),
            P(),
        ),
        check_vma=False,
    )
```

profile of v0, /device:TPU:0, one launch (start us, length us, event | category | flops | bytes accessed | tf_op | source)
XLA Modules:
  0.0 1139.7 jit_solution(12008616428699110538)
XLA Ops:
  7.2 2.6 add_convert_fusion.3
  9.8 2.6 reshape.191
  12.5 4.6 copy.78
  19.6 2.6 reshape.192
  22.2 4.5 copy.76
  29.3 2.6 reshape.193
  31.9 3.5 copy.77
  35.4 3.6 fusion.12
  47.0 4.1 convert_element_type.174
  51.2 2.6 fusion.46
  55.6 23.9 %multiply_convert_fusion.1 = (bf16[640,3072]{1,0:T(8,128)(2,1)S(1)}, f32[640,3072]{1,0:T(8,128)}, f32[640,3072]{1,0:T(8,128)}) fusion(f32[3072]{0:T(1024)S(1)} %copy-done.22, bf16[768,3072]{1,0:T(8,128)(2,1)} %param.30, f32[640,768]{1,0:T(8,128)} %copy-done.8, f32[768]{0:T(1024)S(1)} %copy-done.26, f32[768]{0:T(1024)S(1)} %copy-done.19, ...), kind=kOutput, calls=%fused_computation.7 | convolution fusion | flops 3152117760 | bytes 26369024 | tf_op jit(solution)/shard_map/dot_general | solution.py:131
  79.5 7.2 fusion.47
  90.2 3.3 convert_reduce_fusion.3
  93.5 11.6 %convert_reduce_fusion = (f32[3072]{0:T(1024)S(1)}, bf16[640,3072]{1,0:T(8,128)(2,1)S(1)}) fusion(f32[640,3072]{1,0:T(8,128)} %get-tuple-element.64, bf16[3072,768]{1,0:T(8,128)(2,1)} %param.32, f32[640,768]{1,0:T(8,128)S(1)} %get-tuple-element.60, f32[640,3072]{1,0:T(8,128)} %get-tuple-element.80, f32[3072]{0:T(1024)S(1)} %copy-done.22), kind=kOutput, calls=%fused_computation.2 | convolution fusion | flops 3053810688 | bytes 26370048 | tf_op jit(solution)/shard_map/dot_general | solution.py:36
  105.2 3.8 multiply_reduce_fusion.2
  112.9 4.1 reshape.194
  117.0 4.6 copy.82
  121.6 7.5 multiply_reduce_fusion
  129.1 4.9 multiply_convert_fusion
  138.9 3.6 fusion.26
  145.1 3.5 fusion.25
  151.6 3.6 fusion.27
  157.8 5.5 convert_reduce_fusion.1
  166.5 3.6 fusion.28
  170.1 2.5 copy.104
  172.8 3.3 convolution_convert_fusion.2
  176.2 9.1 convolution_convert_fusion.1
  185.3 8.8 convolution_convert_fusion
  194.3 49.8 %reduce-scatter.19.cloned.1.call-done = bf16[24,768]{1,0:T(8,128)(2,1)} async-done(((bf16[768,768]{1,0:T(8,128)(2,1)}), bf16[24,768]{1,0:T(8,128)(2,1)}) %reduce-scatter.19.cloned.1.call-update) | async-done | bytes 36880 | tf_op jit(solution)/shard_map/reduce_scatter | solution.py:210
  244.2 100.9 %reduce-scatter.21.cloned.1.call-done = bf16[24,768]{1,0:T(8,128)(2,1)} async-done(((bf16[768,768]{1,0:T(8,128)(2,1)}), bf16[24,768]{1,0:T(8,128)(2,1)}) %reduce-scatter.21.cloned.1.call-update) | async-done | bytes 36880 | tf_op jit(solution)/shard_map/reduce_scatter | solution.py:210
  345.1 100.4 %reduce-scatter.23.cloned.1.call-done = bf16[24,768]{1,0:T(8,128)(2,1)} async-done(((bf16[768,768]{1,0:T(8,128)(2,1)}), bf16[24,768]{1,0:T(8,128)(2,1)}) %reduce-scatter.23.cloned.1.call-update) | async-done | bytes 36880 | tf_op jit(solution)/shard_map/reduce_scatter | solution.py:210
  445.6 100.8 %reduce-scatter.13.cloned.1.call-done = bf16[24,768]{1,0:T(8,128)(2,1)} async-done(((bf16[768,768]{1,0:T(8,128)(2,1)}), bf16[24,768]{1,0:T(8,128)(2,1)}) %reduce-scatter.13.cloned.1.call-update) | async-done | bytes 36880 | tf_op jit(solution)/shard_map/reduce_scatter | solution.py:210
  546.4 111.9 %reduce-scatter.15.cloned.1.call-done = bf16[24,3072]{1,0:T(8,128)(2,1)} async-done(((bf16[768,3072]{1,0:T(8,128)(2,1)}), bf16[24,3072]{1,0:T(8,128)(2,1)}) %reduce-scatter.15.cloned.1.call-update) | async-done | bytes 147472 | tf_op jit(solution)/shard_map/reduce_scatter | solution.py:210
  658.4 112.9 %reduce-scatter.17.cloned.1.call-done = bf16[96,768]{1,0:T(8,128)(2,1)} async-done(((bf16[3072,768]{1,0:T(8,128)(2,1)}), bf16[96,768]{1,0:T(8,128)(2,1)}) %reduce-scatter.17.cloned.1.call-update) | async-done | bytes 147472 | tf_op jit(solution)/shard_map/reduce_scatter | solution.py:210
  771.5 40.6 %psum.7 = f32[9216]{0:T(1024)S(1)} all-reduce(f32[9216]{0:T(1024)S(1)} %constant_dynamic-update-slice_fusion), channel_id=1, replica_groups=mesh['dp'=16,'seq'=2] {'dp','seq'}, use_global_device_ids=true, to_apply=%region_21.22 | all-reduce | flops 9216 | bytes 73728 | tf_op jit(solution)/shard_map/psum | solution.py:206
  813.4 2.7 fusion.49
  820.0 7.2 all-gather.7.cloned.1.call-done
  827.3 2.8 convert_element_type.202
  830.1 53.1 %all-gather.9.cloned.1.call-done = bf16[768,768]{1,0:T(8,128)(2,1)} async-done(((bf16[24,768]{1,0:T(8,128)(2,1)}), bf16[768,768]{1,0:T(8,128)(2,1)}) %all-gather.9.cloned.1.call-update) | async-done | bytes 1179664 | tf_op jit(solution)/shard_map/all_gather | solution.py:213
  883.2 2.8 convert_element_type.210
  886.0 53.1 %all-gather.11.cloned.1.call-done = bf16[768,768]{1,0:T(8,128)(2,1)} async-done(((bf16[24,768]{1,0:T(8,128)(2,1)}), bf16[768,768]{1,0:T(8,128)(2,1)}) %all-gather.11.cloned.1.call-update) | async-done | bytes 1179664 | tf_op jit(solution)/shard_map/all_gather | solution.py:213
  939.1 2.8 convert_element_type.213
  941.9 52.9 %all-gather.13.cloned.1.call-done = bf16[768,768]{1,0:T(8,128)(2,1)} async-done(((bf16[24,768]{1,0:T(8,128)(2,1)}), bf16[768,768]{1,0:T(8,128)(2,1)}) %all-gather.13.cloned.1.call-update) | async-done | bytes 1179664 | tf_op jit(solution)/shard_map/all_gather | solution.py:213
  994.8 2.8 convert_element_type.215
  997.7 62.7 %all-gather.15.cloned.1.call-done = bf16[768,3072]{1,0:T(8,128)(2,1)} async-done(((bf16[24,3072]{1,0:T(8,128)(2,1)}), bf16[768,3072]{1,0:T(8,128)(2,1)}) %all-gather.15.cloned.1.call-update) | async-done | bytes 4718608 | tf_op jit(solution)/shard_map/all_gather | solution.py:213
  1060.4 7.4 convert_element_type.217
  1067.7 57.9 %all-gather.17.cloned.1.call-done = bf16[3072,768]{1,0:T(8,128)(2,1)} async-done(((bf16[96,768]{1,0:T(8,128)(2,1)}), bf16[3072,768]{1,0:T(8,128)(2,1)}) %all-gather.17.cloned.1.call-update) | async-done | bytes 4718608 | tf_op jit(solution)/shard_map/all_gather | solution.py:213
  1125.6 6.8 convert_element_type.219
  (134 shorter events, 44.2 us)
Async XLA Ops:
  7.2 43.9 %copy-start = (bf16[768,768]{1,0:T(8,128)(2,1)S(1)}, bf16[768,768]{1,0:T(8,128)(2,1)}, u32[]{:S(2)}) copy-start(bf16[768,768]{1,0:T(8,128)(2,1)} %param.26) | copy-start | bytes 3538948
  7.2 236.9 %reduce-scatter.19.cloned.1.call-start = ((), (), s32[]{:S(2)}) async-start(), calls=%async_computation.15 | async-start | bytes 1216512 | tf_op jit(solution)/shard_map/reduce_scatter | solution.py:210
  12.5 4.6 copy-start.20
  12.5 4.6 copy-start.23
  39.0 3.2 copy-start.1
  39.0 3.2 copy-start.11
  44.6 6.5 copy-start.24
  51.1 4.4 copy-start.19
  51.1 4.4 copy-start.22
  51.1 4.4 copy-start.26
  53.8 1.3 copy-start.8
  55.5 24.0 %copy-start.9 = (f32[640,768]{1,0:T(8,128)S(1)}, f32[640,768]{1,0:T(8,128)}, u32[]{:S(2)}) copy-start(f32[640,768]{1,0:T(8,128)} %copy-done.8) | copy-start | bytes 5898244
  55.5 24.0 %copy-start.25 = (f32[768]{0:T(1024)S(1)}, f32[768]{0:T(1024)}, u32[]{:S(2)}) copy-start(f32[768]{0:T(1024)} %param.33) | copy-start | bytes 9220
  79.5 7.2 copy-start.27
  79.5 7.6 copy-start.17
  86.7 3.3 copy-start.3
  86.7 1.9 copy-start.5
  87.1 3.0 copy-start.18
  90.2 15.0 %slice-start = ((s8[4718592]{0:T(1024)(128)(4,1)}), s8[4194304]{0:T(1024)(128)(4,1)S(1)}, s32[]{:S(2)}) async-start(s8[4718592]{0:T(1024)(128)(4,1)} %bitcast.81), calls=%async_computation.18 | async-start | bytes 8388608
  93.5 11.7 %copy-start.14 = (f32[640,768]{1,0:T(8,128)}, f32[640,768]{1,0:T(8,128)S(1)}, u32[]{:S(2)}) copy-start(f32[640,768]{1,0:T(8,128)S(1)} %get-tuple-element.60) | copy-start | bytes 5898244
  93.5 11.7 %copy-start.10 = (f32[640,768]{1,0:T(8,128)S(1)}, f32[640,768]{1,0:T(8,128)}, u32[]{:S(2)}) copy-start(f32[640,768]{1,0:T(8,128)} %copy-done.8) | copy-start | bytes 5898244
  93.5 11.7 %slice-start.1 = ((s8[4718592]{0:T(1024)(128)(4,1)}), s8[524288]{0:T(1024)(128)(4,1)S(1)}, s32[]{:S(2)}) async-start(s8[4718592]{0:T(1024)(128)(4,1)} %bitcast.81), calls=%async_computation.19 | async-start | bytes 1048576
  105.1 3.9 copy-start.28
  109.7 1.3 copy-start.6
  134.0 1.9 copy-start.2
  142.5 2.6 copy-start.4
  145.0 200.0 %reduce-scatter.21.cloned.1.call-start = ((), (), s32[]{:S(2)}) async-start(), calls=%async_computation.16 | async-start | bytes 1216512 | tf_op jit(solution)/shard_map/reduce_scatter | solution.py:210
  155.2 2.6 copy-start.12
  157.7 287.8 %reduce-scatter.23.cloned.1.call-start = ((), (), s32[]{:S(2)}) async-start(), calls=%async_computation.17 | async-start | bytes 1216512 | tf_op jit(solution)/shard_map/reduce_scatter | solution.py:210
  170.1 2.6 copy-start.7
  172.7 373.6 %reduce-scatter.13.cloned.1.call-start = ((), (), s32[]{:S(2)}) async-start(), calls=%async_computation.9 | async-start | bytes 1216512 | tf_op jit(solution)/shard_map/reduce_scatter | solution.py:210
  176.1 482.2 %reduce-scatter.15.cloned.1.call-start = ((), (), s32[]{:S(2)}) async-start(), calls=%async_computation.11 | async-start | bytes 4866048 | tf_op jit(solution)/shard_map/reduce_scatter | solution.py:210
  185.3 585.9 %reduce-scatter.17.cloned.1.call-start = ((), (), s32[]{:S(2)}) async-start(), calls=%async_computation.13 | async-start | bytes 4866048 | tf_op jit(solution)/shard_map/reduce_scatter | solution.py:210
  194.2 633.1 %all-gather.7.cloned.1.call-start = ((), (), s32[]{:S(2)}) async-start(), calls=%async_computation.6 | async-start | bytes 1216512 | tf_op jit(solution)/shard_map/all_gather | solution.py:213
  244.1 639.1 %all-gather.9.cloned.1.call-start = ((), (), s32[]{:S(2)}) async-start(), calls=%async_computation.7 | async-start | bytes 1216512 | tf_op jit(solution)/shard_map/all_gather | solution.py:213
  345.0 594.0 %all-gather.11.cloned.1.call-start = ((), (), s32[]{:S(2)}) async-start(), calls=%async_computation.8 | async-start | bytes 1216512 | tf_op jit(solution)/shard_map/all_gather | solution.py:213
  445.5 549.3 %all-gather.13.cloned.1.call-start = ((), (), s32[]{:S(2)}) async-start(), calls=%async_computation.10 | async-start | bytes 1216512 | tf_op jit(solution)/shard_map/all_gather | solution.py:213
  546.3 514.0 %all-gather.15.cloned.1.call-start = ((), (), s32[]{:S(2)}) async-start(), calls=%async_computation.12 | async-start | bytes 4866048 | tf_op jit(solution)/shard_map/all_gather | solution.py:213
  658.3 467.3 %all-gather.17.cloned.1.call-start = ((), (), s32[]{:S(2)}) async-start(), calls=%async_computation.14 | async-start | bytes 4866048 | tf_op jit(solution)/shard_map/all_gather | solution.py:213
  812.7 3.4 copy-start.16
  812.7 3.4 copy-start.21
  816.1 1.2 copy-start.13
  816.1 1.6 copy-start.15
Sparse Core Ops, SparseCore 0:
  145.2 98.8 reduce-scatter.18
  249.7 95.2 reduce-scatter.20
  350.1 95.3 reduce-scatter.22
  451.0 95.2 reduce-scatter.12
  552.2 106.0 reduce-scatter.14
  665.1 106.0 reduce-scatter.16
  774.1 53.1 all-gather.6
  830.2 52.9 all-gather.8
  886.1 52.9 all-gather.10
  941.8 52.9 all-gather.12
  997.7 62.5 all-gather.14
  1063.1 62.4 all-gather.16
where the time goes:
time: 1150 us; the launch traced here: 1140 us
  waiting for transfers between devices  864 us (75%)
  matrix products  120 us (10%)
  local copies, waits for them, and re-layouts  60.8 us (5%)
  blocking collectives  40.6 us (4%)
  other arithmetic  38.7 us (3%)
  between operations  15.3 us (1%)
    reduce_scatter x6, waiting for transfers between devices, body(): lax.psum_scatter(grad.astype(low_type), ('dp', 'seq'), scatter_dimension=...  577 us
    all_gather x6, waiting for transfers between devices, body(): lax.all_gather(part, ('dp', 'seq'), axis=0, tiled=True).astype(f32)  287 us
    psum x1, blocking collectives, body(): sums = lax.psum(jnp.concatenate(small), ('dp', 'seq'))  40.6 us
    dot_general x6, matrix products, over_rows(): lax.dot_general(left, right, (((0,), (0,)), ((), ())), preferred_element_...  32.1 us
    convert_element_type x6, other arithmetic, body(): lax.all_gather(part, ('dp', 'seq'), axis=0, tiled=True).astype(f32)  25.6 us
    dot_general x1, matrix products, body(): pre = jnp.dot(fin, w_inner, preferred_element_type=f32) + b_inner  23.9 us
    dot_general x6, matrix products, times_trans(): lax.dot_general(left, weight, (((1,), (1,)), ((), ())), preferred_element...  23.5 us
  transfers between devices with their start and end apart: 12, of which 12 were waited for; matrix products, arithmetic and copies ran while one was open for 7% of the time, Pallas kernels for 0%

commit v1 on v0

--- a/solution.py
+++ b/solution.py
@@ -5,6 +5,29 @@
 
 H = 12
 EPS = 1e-12
+
+
+def in_order(blocks, dim):
+    shape = list(blocks.shape[1:])
+    shape[dim] *= blocks.shape[0]
+    return jnp.moveaxis(blocks, 0, dim).reshape(shape)
+
+
+def doubled(array, axis):
+    length, mine = (lax.axis_size(axis), lax.axis_index(axis))
+    blocks, distance = (array[None], 1)
+    while distance < length:
+        received = lax.ppermute(blocks, axis, [(i, i ^ distance) for i in range(length)])
+        low = mine & distance == 0
+        blocks = jnp.concatenate(
+            [jnp.where(low, blocks, received), jnp.where(low, received, blocks)]
+        )
+        distance *= 2
+    return blocks
+
+
+def collect(shard, axis, dim):
+    return in_order(doubled(shard, axis), dim)
 
 
 def norm_forward(h, gain, shift):
@@ -210,7 +233,7 @@
         part = lax.psum_scatter(
             grad.astype(low_type), ("dp", "seq"), scatter_dimension=0, tiled=True
         )
-        big_sums.append(lax.all_gather(part, ("dp", "seq"), axis=0, tiled=True).astype(f32))
+        big_sums.append(collect(part, ("dp", "seq"), 0).astype(f32))
     every = []
     for grad in local_grads:
         every.append(big_sums.pop(0) if grad.ndim == 2 else small_sums[0])

time: 1150 us -> 1040 us (0.904)
  waiting for transfers between devices: 864 us -> 708 us
  starting transfers between devices: 0.48 us -> 33.9 us
    reduce_scatter x6 -> x2, waiting for transfers between devices: 577 us -> 147 us  [body(): lax.psum_scatter(grad.astype(low_type), ('dp', 'seq'), scatter_dimension=...]
    unnamed x12 -> x10, waiting for transfers between devices: 0.2 us -> 296 us
    all_gather x6 -> x0, waiting for transfers between devices: 287 us -> none  [body(): lax.all_gather(part, ('dp', 'seq'), axis=0, tiled=True).astype(f32)]
    ppermute x0 -> x30, waiting for transfers between devices: none -> 264 us  [doubled(): lax.ppermute(blocks, axis, [(i, i ^ distance) for i in range(length)])]
    ppermute x0 -> x30, starting transfers between devices: none -> 33.3 us  [doubled(): lax.ppermute(blocks, axis, [(i, i ^ distance) for i in range(length)])]
  transfers between devices with their start and end apart: 12 -> 36, of which waited for: 12 -> 18; matrix products, arithmetic and copies ran while one was open for 7% -> 9% of each run, Pallas kernels for 0% -> 0%
where the time goes in v1:
time: 1040 us; the launch traced here: 1030 us
  waiting for transfers between devices  708 us (68%)
  matrix products  123 us (12%)
  local copies, waits for them, and re-layouts  61.7 us (6%)
  other arithmetic  44 us (4%)
  blocking collectives  42.7 us (4%)
  starting transfers between devices  33.9 us (3%)
  between operations  15.6 us (2%)
    unnamed x10, waiting for transfers between devices  296 us
    ppermute x30, waiting for transfers between devices, doubled(): lax.ppermute(blocks, axis, [(i, i ^ distance) for i in range(length)])  264 us
    reduce_scatter x2, waiting for transfers between devices, body(): lax.psum_scatter(grad.astype(low_type), ('dp', 'seq'), scatter_dimension=...  147 us
    psum x1, blocking collectives, body(): sums = lax.psum(jnp.concatenate(small), ('dp', 'seq'))  42.7 us
    ppermute x30, starting transfers between devices, doubled(): lax.ppermute(blocks, axis, [(i, i ^ distance) for i in range(length)])  33.3 us
    dot_general x6, matrix products, over_rows(): lax.dot_general(left, right, (((0,), (0,)), ((), ())), preferred_element_...  29.8 us
    dot_general x6, matrix products, times_trans(): lax.dot_general(left, weight, (((1,), (1,)), ((), ())), preferred_element...  28.1 us
    dot_general x1, matrix products, body(): pre = jnp.dot(fin, w_inner, preferred_element_type=f32) + b_inner  23.9 us
  transfers between devices with their start and end apart: 36, of which 18 were waited for; matrix products, arithmetic and copies ran while one was open for 9% of the time, Pallas kernels for 0%

profile of v1, /device:TPU:0, one launch (start us, length us, event | category | flops | bytes accessed | tf_op | source)
XLA Modules:
  0.0 1028.4 jit_solution(13648942431396842699)
XLA Ops:
  7.3 2.6 add_convert_fusion.3
  9.8 2.6 reshape.217
  12.5 4.6 copy.78
  17.1 2.5 add_convert_fusion.2
  19.6 2.6 reshape.218
  22.2 4.5 copy.76
  29.3 2.6 reshape.219
  31.9 3.5 copy.77
  35.4 3.6 fusion.12
  47.0 4.0 convert_element_type.192
  51.1 2.6 fusion.46
  55.5 23.9 %multiply_convert_fusion.1 = (bf16[640,3072]{1,0:T(8,128)(2,1)S(1)}, f32[640,3072]{1,0:T(8,128)}, f32[640,3072]{1,0:T(8,128)}) fusion(f32[3072]{0:T(1024)S(1)} %copy-done.25, bf16[768,3072]{1,0:T(8,128)(2,1)} %param.30, f32[640,768]{1,0:T(8,128)} %copy-done.9, f32[768]{0:T(1024)S(1)} %copy-done.29, f32[768]{0:T(1024)S(1)} %copy-done.22, ...), kind=kOutput, calls=%fused_computation.7 | convolution fusion | flops 3152117760 | bytes 26369024 | tf_op jit(solution)/shard_map/dot_general | solution.py:154
  79.5 7.2 fusion.47
  90.1 3.3 convert_reduce_fusion.3
  93.4 11.3 %convert_reduce_fusion = (f32[3072]{0:T(1024)S(1)}, bf16[640,3072]{1,0:T(8,128)(2,1)S(1)}) fusion(f32[640,3072]{1,0:T(8,128)} %get-tuple-element.30, bf16[3072,768]{1,0:T(8,128)(2,1)} %param.32, f32[640,768]{1,0:T(8,128)S(1)} %get-tuple-element.26, f32[640,3072]{1,0:T(8,128)} %get-tuple-element.106, f32[3072]{0:T(1024)S(1)} %copy-done.25), kind=kOutput, calls=%fused_computation.2 | convolution fusion | flops 3053810688 | bytes 26370048 | tf_op jit(solution)/shard_map/dot_general | solution.py:59
  104.8 3.8 multiply_reduce_fusion.2
  112.6 4.1 reshape.220
  116.7 4.5 copy.82
  121.2 7.5 multiply_reduce_fusion
  128.7 5.1 multiply_convert_fusion
  138.8 2.6 fusion.26
  142.9 3.5 fusion.25
  149.4 2.6 fusion.27
  153.7 5.5 convert_reduce_fusion.1
  161.5 3.3 fusion.28
  164.8 2.5 copy.110
  167.4 3.3 convolution_convert_fusion.2
  170.8 9.1 convolution_convert_fusion.1
  180.2 8.9 convolution_convert_fusion
  189.1 4.0 fusion.49
  195.6 42.7 %psum.7 = f32[9216]{0:T(1024)S(1)} all-reduce(f32[9216]{0:T(1024)S(1)} %constant_dynamic-update-slice_fusion), channel_id=1, replica_groups=mesh['dp'=16,'seq'=2] {'dp','seq'}, use_global_device_ids=true, to_apply=%region_21.22 | all-reduce | flops 9216 | bytes 73728 | tf_op jit(solution)/shard_map/psum | solution.py:229
  238.3 4.8 add_add_fusion
  245.3 97.6 %reduce-scatter.21.cloned.1.call-done = bf16[24,768]{1,0:T(8,128)(2,1)} async-done(((bf16[768,768]{1,0:T(8,128)(2,1)}), bf16[24,768]{1,0:T(8,128)(2,1)}) %reduce-scatter.21.cloned.1.call-update) | async-done | bytes 36880
  343.9 99.4 %reduce-scatter.23.cloned.1.call-done = bf16[24,768]{1,0:T(8,128)(2,1)} async-done(((bf16[768,768]{1,0:T(8,128)(2,1)}), bf16[24,768]{1,0:T(8,128)(2,1)}) %reduce-scatter.23.cloned.1.call-update) | async-done | bytes 36880
  444.4 99.3 %reduce-scatter.25.cloned.1.call-done = bf16[24,768]{1,0:T(8,128)(2,1)} async-done(((bf16[768,768]{1,0:T(8,128)(2,1)}), bf16[24,768]{1,0:T(8,128)(2,1)}) %reduce-scatter.25.cloned.1.call-update) | async-done | bytes 36880
  568.8 19.4 %collective-permute-done.8 = bf16[8,24,768]{2,1,0:T(8,128)(2,1)S(1)} collective-permute-done((bf16[8,24,768]{2,1,0:T(8,128)(2,1)S(1)}, bf16[8,24,768]{2,1,0:T(8,128)(2,1)S(1)}, u32[]{:S(2)}, u32[]{:S(2)}) %collective-permute-start.8) | collective-permute-done | bytes 294944 | tf_op jit(solution)/shard_map/ppermute | solution.py:20
  589.1 78.0 %reduce-scatter.15.cloned.1.call-done = bf16[24,3072]{1,0:T(8,128)(2,1)} async-done(((bf16[768,3072]{1,0:T(8,128)(2,1)}), bf16[24,3072]{1,0:T(8,128)(2,1)}) %reduce-scatter.15.cloned.1.call-update) | async-done | bytes 147472 | tf_op jit(solution)/shard_map/reduce_scatter | solution.py:233
  674.7 4.4 collective-permute-done.21
  683.7 26.9 %collective-permute-done.14 = bf16[16,24,768]{2,1,0:T(8,128)(2,1)S(1)} collective-permute-done((bf16[16,24,768]{2,1,0:T(8,128)(2,1)S(1)}, bf16[16,24,768]{2,1,0:T(8,128)(2,1)S(1)}, u32[]{:S(2)}, u32[]{:S(2)}) %collective-permute-start.14) | collective-permute-done | bytes 589856 | tf_op jit(solution)/shard_map/ppermute | solution.py:20
  710.7 69.3 %reduce-scatter.17.cloned.1.call-done = bf16[96,768]{1,0:T(8,128)(2,1)} async-done(((bf16[3072,768]{1,0:T(8,128)(2,1)}), bf16[96,768]{1,0:T(8,128)(2,1)}) %reduce-scatter.17.cloned.1.call-update) | async-done | bytes 147472 | tf_op jit(solution)/shard_map/reduce_scatter | solution.py:233
  785.8 6.3 collective-permute-done.26
  793.8 16.0 %collective-permute-done.23 = bf16[8,24,3072]{2,1,0:T(8,128)(2,1)S(1)} collective-permute-done((bf16[8,24,3072]{2,1,0:T(8,128)(2,1)S(1)}, bf16[8,24,3072]{2,1,0:T(8,128)(2,1)S(1)}, u32[]{:S(2)}, u32[]{:S(2)}) %collective-permute-start.23) | collective-permute-done | bytes 1179680 | tf_op jit(solution)/shard_map/ppermute | solution.py:20
  818.6 68.9 %collective-permute-done.28 = bf16[8,96,768]{2,1,0:T(8,128)(2,1)S(1)} collective-permute-done((bf16[8,96,768]{2,1,0:T(8,128)(2,1)S(1)}, bf16[8,96,768]{2,1,0:T(8,128)(2,1)S(1)}, u32[]{:S(2)}, u32[]{:S(2)}) %collective-permute-start.28) | collective-permute-done | bytes 1179680 | tf_op jit(solution)/shard_map/ppermute | solution.py:20
  887.8 3.2 collective-permute-start.29
  892.7 73.3 %collective-permute-done.24 = bf16[16,24,3072]{2,1,0:T(8,128)(2,1)S(1)} collective-permute-done((bf16[16,24,3072]{2,1,0:T(8,128)(2,1)S(1)}, bf16[16,24,3072]{2,1,0:T(8,128)(2,1)S(1)}, u32[]{:S(2)}, u32[]{:S(2)}) %collective-permute-start.24) | collective-permute-done | bytes 2359328 | tf_op jit(solution)/shard_map/ppermute | solution.py:20
  966.7 5.3 bitcast_convert_fusion.1
  972.0 43.6 %collective-permute-done.29 = bf16[16,96,768]{2,1,0:T(8,128)(2,1)S(1)} collective-permute-done((bf16[16,96,768]{2,1,0:T(8,128)(2,1)S(1)}, bf16[16,96,768]{2,1,0:T(8,128)(2,1)S(1)}, u32[]{:S(2)}, u32[]{:S(2)}) %collective-permute-start.29) | collective-permute-done | bytes 2359328 | tf_op jit(solution)/shard_map/ppermute | solution.py:20
  1016.3 4.8 bitcast_convert_fusion
  (254 shorter events, 97.7 us)
Async XLA Ops:
  7.2 43.9 %copy-start = (bf16[768,768]{1,0:T(8,128)(2,1)S(1)}, bf16[768,768]{1,0:T(8,128)(2,1)}, u32[]{:S(2)}) copy-start(bf16[768,768]{1,0:T(8,128)(2,1)} %param.26) | copy-start | bytes 3538948
  7.2 235.8 %reduce-scatter.19.cloned.1.call-start = ((), (), s32[]{:S(2)}) async-start(), calls=%async_computation.8 | async-start | bytes 1216512
  12.5 4.6 copy-start.26
  44.6 6.4 copy-start.27
  55.5 24.0 %copy-start.10 = (f32[640,768]{1,0:T(8,128)S(1)}, f32[640,768]{1,0:T(8,128)}, u32[]{:S(2)}) copy-start(f32[640,768]{1,0:T(8,128)} %copy-done.9) | copy-start | bytes 5898244
  55.5 24.0 %copy-start.28 = (f32[768]{0:T(1024)S(1)}, f32[768]{0:T(1024)}, u32[]{:S(2)}) copy-start(f32[768]{0:T(1024)} %param.33) | copy-start | bytes 9220
  79.4 7.2 copy-start.30
  79.5 7.6 copy-start.20
  90.1 14.7 %slice-start = ((s8[4718592]{0:T(1024)(128)(4,1)}), s8[4194304]{0:T(1024)(128)(4,1)S(1)}, s32[]{:S(2)}) async-start(s8[4718592]{0:T(1024)(128)(4,1)} %bitcast.124), calls=%async_computation.12 | async-start | bytes 8388608
  93.4 11.4 %copy-start.16 = (f32[640,768]{1,0:T(8,128)}, f32[640,768]{1,0:T(8,128)S(1)}, u32[]{:S(2)}) copy-start(f32[640,768]{1,0:T(8,128)S(1)} %get-tuple-element.26) | copy-start | bytes 5898244
  93.4 11.4 %copy-start.11 = (f32[640,768]{1,0:T(8,128)S(1)}, f32[640,768]{1,0:T(8,128)}, u32[]{:S(2)}) copy-start(f32[640,768]{1,0:T(8,128)} %copy-done.9) | copy-start | bytes 5898244
  93.4 11.4 %slice-start.1 = ((s8[4718592]{0:T(1024)(128)(4,1)}), s8[524288]{0:T(1024)(128)(4,1)S(1)}, s32[]{:S(2)}) async-start(s8[4718592]{0:T(1024)(128)(4,1)} %bitcast.124), calls=%async_computation.13 | async-start | bytes 1048576
  142.9 200.1 %reduce-scatter.21.cloned.1.call-start = ((), (), s32[]{:S(2)}) async-start(), calls=%async_computation.9 | async-start | bytes 1216512
  153.5 289.9 %reduce-scatter.23.cloned.1.call-start = ((), (), s32[]{:S(2)}) async-start(), calls=%async_computation.10 | async-start | bytes 1216512
  167.4 376.3 %reduce-scatter.25.cloned.1.call-start = ((), (), s32[]{:S(2)}) async-start(), calls=%async_computation.11 | async-start | bytes 1216512
  170.8 496.4 %reduce-scatter.15.cloned.1.call-start = ((), (), s32[]{:S(2)}) async-start(), calls=%async_computation.6 | async-start | bytes 4866048 | tf_op jit(solution)/shard_map/reduce_scatter | solution.py:233
  179.9 600.1 %reduce-scatter.17.cloned.1.call-start = ((), (), s32[]{:S(2)}) async-start(), calls=%async_computation.7 | async-start | bytes 4866048 | tf_op jit(solution)/shard_map/reduce_scatter | solution.py:233
  244.0 300.7 %collective-permute-start = (bf16[1,24,768]{1,2,0:T(8,128)(2,1)S(1)}, bf16[1,24,768]{1,2,0:T(8,128)(2,1)S(1)}, u32[]{:S(2)}, u32[]{:S(2)}) collective-permute-start(bf16[1,24,768]{1,2,0:T(8,128)(2,1)S(1)} %bitcast.118), channel_id=1, source_target_pairs={{0,1},{1,0},{2,3},{3,2},{4,5},{5,4},{6,7},{7,6},{8,9},{9,8},{10,11... | collective-permute-start | bytes 110600 | tf_op jit(solution)/shard_map/ppermute | solution.py:20
  343.9 202.6 %collective-permute-start.5 = (bf16[1,24,768]{1,2,0:T(8,128)(2,1)S(1)}, bf16[1,24,768]{1,2,0:T(8,128)(2,1)S(1)}, u32[]{:S(2)}, u32[]{:S(2)}) collective-permute-start(bf16[1,24,768]{1,2,0:T(8,128)(2,1)S(1)} %bitcast.121), channel_id=1, source_target_pairs={{0,1},{1,0},{2,3},{3,2},{4,5},{5,4},{6,7},{7,6},{8,9},{9,8},{10,11... | collective-permute-start | bytes 110600 | tf_op jit(solution)/shard_map/ppermute | solution.py:20
  444.3 103.1 %collective-permute-start.10 = (bf16[1,24,768]{1,2,0:T(8,128)(2,1)S(1)}, bf16[1,24,768]{1,2,0:T(8,128)(2,1)S(1)}, u32[]{:S(2)}, u32[]{:S(2)}) collective-permute-start(bf16[1,24,768]{1,2,0:T(8,128)(2,1)S(1)} %bitcast.120), channel_id=1, source_target_pairs={{0,1},{1,0},{2,3},{3,2},{4,5},{5,4},{6,7},{7,6},{8,9},{9,8},{10,11... | collective-permute-start | bytes 110600 | tf_op jit(solution)/shard_map/ppermute | solution.py:20
  544.6 4.6 collective-permute-start.15
  545.0 5.2 collective-permute-start.1
  546.8 5.2 collective-permute-start.6
  547.7 5.8 collective-permute-start.11
  549.5 5.6 collective-permute-start.16
  550.2 6.8 collective-permute-start.2
  552.0 8.3 collective-permute-start.7
  553.6 9.7 collective-permute-start.12
  555.1 10.3 %collective-permute-start.17 = (bf16[4,24,768]{2,1,0:T(8,128)(2,1)S(1)}, bf16[4,24,768]{2,1,0:T(8,128)(2,1)S(1)}, u32[]{:S(2)}, u32[]{:S(2)}) collective-permute-start(bf16[4,24,768]{2,1,0:T(8,128)(2,1)S(1)} %pad_maximum_fusion.25), channel_id=1, source_target_pairs={{0,4},{1,5},{2,6},{3,7},{4,0},{5,1},{6,2},{7,3},{8,12},{9,13},{10,... | collective-permute-start | bytes 442376 | tf_op jit(solution)/shard_map/ppermute | solution.py:20
  557.1 10.0 collective-permute-start.3
  560.3 27.9 %collective-permute-start.8 = (bf16[8,24,768]{2,1,0:T(8,128)(2,1)S(1)}, bf16[8,24,768]{2,1,0:T(8,128)(2,1)S(1)}, u32[]{:S(2)}, u32[]{:S(2)}) collective-permute-start(bf16[8,24,768]{2,1,0:T(8,128)(2,1)S(1)} %pad_maximum_fusion.17), channel_id=1, source_target_pairs={{0,8},{1,9},{2,10},{3,11},{4,12},{5,13},{6,14},{7,15},{8,0},{9,1},... | collective-permute-start | bytes 884744 | tf_op jit(solution)/shard_map/ppermute | solution.py:20
  564.1 103.1 %collective-permute-start.13 = (bf16[8,24,768]{2,1,0:T(8,128)(2,1)}, bf16[8,24,768]{2,1,0:T(8,128)(2,1)}, u32[]{:S(2)}, u32[]{:S(2)}) collective-permute-start(bf16[8,24,768]{2,1,0:T(8,128)(2,1)} %pad_maximum_fusion.18), channel_id=1, source_target_pairs={{0,8},{1,9},{2,10},{3,11},{4,12},{5,13},{6,14},{7,15},{8,0},{9,1},... | collective-permute-start | bytes 884744 | tf_op jit(solution)/shard_map/ppermute | solution.py:20
  565.5 105.9 %collective-permute-start.18 = (bf16[8,24,768]{2,1,0:T(8,128)(2,1)S(1)}, bf16[8,24,768]{2,1,0:T(8,128)(2,1)}, u32[]{:S(2)}, u32[]{:S(2)}) collective-permute-start(bf16[8,24,768]{2,1,0:T(8,128)(2,1)S(1)} %pad_maximum_fusion.19), channel_id=1, source_target_pairs={{0,8},{1,9},{2,10},{3,11},{4,12},{5,13},{6,14},{7,15},{8,0},{9,1},... | collective-permute-start | bytes 884744 | tf_op jit(solution)/shard_map/ppermute | solution.py:20
  567.3 114.2 %collective-permute-start.4 = (bf16[16,24,768]{2,1,0:T(8,128)(2,1)S(1)}, bf16[16,24,768]{2,1,0:T(8,128)(2,1)S(1)}, u32[]{:S(2)}, u32[]{:S(2)}) collective-permute-start(bf16[16,24,768]{2,1,0:T(8,128)(2,1)S(1)} %pad_maximum_fusion.10), channel_id=1, source_target_pairs={{0,16},{1,17},{2,18},{3,19},{4,20},{5,21},{6,22},{7,23},{8,24},{9,... | collective-permute-start | bytes 1769480 | tf_op jit(solution)/shard_map/ppermute | solution.py:20
  589.1 93.4 %collective-permute-start.9 = (bf16[16,24,768]{2,1,0:T(8,128)(2,1)}, bf16[16,24,768]{2,1,0:T(8,128)(2,1)}, u32[]{:S(2)}, u32[]{:S(2)}) collective-permute-start(bf16[16,24,768]{2,1,0:T(8,128)(2,1)} %pad_maximum_fusion.11), channel_id=1, source_target_pairs={{0,16},{1,17},{2,18},{3,19},{4,20},{5,21},{6,22},{7,23},{8,24},{9,... | collective-permute-start | bytes 1769480 | tf_op jit(solution)/shard_map/ppermute | solution.py:20
  667.1 2.7 collective-permute-start.20
  668.3 42.4 %collective-permute-start.14 = (bf16[16,24,768]{2,1,0:T(8,128)(2,1)S(1)}, bf16[16,24,768]{2,1,0:T(8,128)(2,1)S(1)}, u32[]{:S(2)}, u32[]{:S(2)}) collective-permute-start(bf16[16,24,768]{2,1,0:T(8,128)(2,1)S(1)} %pad_maximum_fusion.12), channel_id=1, source_target_pairs={{0,16},{1,17},{2,18},{3,19},{4,20},{5,21},{6,22},{7,23},{8,24},{9,... | collective-permute-start | bytes 1769480 | tf_op jit(solution)/shard_map/ppermute | solution.py:20
  669.9 9.2 collective-permute-start.21
  673.3 111.4 %collective-permute-start.19 = (bf16[16,24,768]{2,1,0:T(8,128)(2,1)}, bf16[16,24,768]{2,1,0:T(8,128)(2,1)}, u32[]{:S(2)}, u32[]{:S(2)}) collective-permute-start(bf16[16,24,768]{2,1,0:T(8,128)(2,1)} %pad_maximum_fusion.13), channel_id=1, source_target_pairs={{0,16},{1,17},{2,18},{3,19},{4,20},{5,21},{6,22},{7,23},{8,24},{9,... | collective-permute-start | bytes 1769480 | tf_op jit(solution)/shard_map/ppermute | solution.py:20
  680.0 100.0 %collective-permute-start.22 = (bf16[4,24,3072]{2,1,0:T(8,128)(2,1)}, bf16[4,24,3072]{2,1,0:T(8,128)(2,1)}, u32[]{:S(2)}, u32[]{:S(2)}) collective-permute-start(bf16[4,24,3072]{2,1,0:T(8,128)(2,1)} %pad_maximum_fusion.14), channel_id=1, source_target_pairs={{0,4},{1,5},{2,6},{3,7},{4,0},{5,1},{6,2},{7,3},{8,12},{9,13},{10,... | collective-permute-start | bytes 1769480 | tf_op jit(solution)/shard_map/ppermute | solution.py:20
  780.1 2.9 collective-permute-start.25
  781.4 28.4 %collective-permute-start.23 = (bf16[8,24,3072]{2,1,0:T(8,128)(2,1)S(1)}, bf16[8,24,3072]{2,1,0:T(8,128)(2,1)S(1)}, u32[]{:S(2)}, u32[]{:S(2)}) collective-permute-start(bf16[8,24,3072]{2,1,0:T(8,128)(2,1)S(1)} %pad_maximum_fusion.8), channel_id=1, source_target_pairs={{0,8},{1,9},{2,10},{3,11},{4,12},{5,13},{6,14},{7,15},{8,0},{9,1},... | collective-permute-start | bytes 3538952 | tf_op jit(solution)/shard_map/ppermute | solution.py:20
  783.0 9.1 collective-permute-start.26
  792.3 19.5 %collective-permute-start.27 = (bf16[4,96,768]{2,1,0:T(8,128)(2,1)S(1)}, bf16[4,96,768]{2,1,0:T(8,128)(2,1)S(1)}, u32[]{:S(2)}, u32[]{:S(2)}) collective-permute-start(bf16[4,96,768]{2,1,0:T(8,128)(2,1)S(1)} %pad_maximum_fusion.15), channel_id=1, source_target_pairs={{0,4},{1,5},{2,6},{3,7},{4,0},{5,1},{6,2},{7,3},{8,12},{9,13},{10,... | collective-permute-start | bytes 1769480 | tf_op jit(solution)/shard_map/ppermute | solution.py:20
  810.2 155.8 %collective-permute-start.24 = (bf16[16,24,3072]{2,1,0:T(8,128)(2,1)S(1)}, bf16[16,24,3072]{2,1,0:T(8,128)(2,1)S(1)}, u32[]{:S(2)}, u32[]{:S(2)}) collective-permute-start(bf16[16,24,3072]{2,1,0:T(8,128)(2,1)S(1)} %pad_maximum_fusion.2), channel_id=1, source_target_pairs={{0,16},{1,17},{2,18},{3,19},{4,20},{5,21},{6,22},{7,23},{8,24},{9,... | collective-permute-start | bytes 7077896 | tf_op jit(solution)/shard_map/ppermute | solution.py:20
  812.0 75.4 %collective-permute-start.28 = (bf16[8,96,768]{2,1,0:T(8,128)(2,1)S(1)}, bf16[8,96,768]{2,1,0:T(8,128)(2,1)S(1)}, u32[]{:S(2)}, u32[]{:S(2)}) collective-permute-start(bf16[8,96,768]{2,1,0:T(8,128)(2,1)S(1)} %pad_maximum_fusion.9), channel_id=1, source_target_pairs={{0,8},{1,9},{2,10},{3,11},{4,12},{5,13},{6,14},{7,15},{8,0},{9,1},... | collective-permute-start | bytes 3538952 | tf_op jit(solution)/shard_map/ppermute | solution.py:20
  887.8 127.8 %collective-permute-start.29 = (bf16[16,96,768]{2,1,0:T(8,128)(2,1)S(1)}, bf16[16,96,768]{2,1,0:T(8,128)(2,1)S(1)}, u32[]{:S(2)}, u32[]{:S(2)}) collective-permute-start(bf16[16,96,768]{2,1,0:T(8,128)(2,1)S(1)} %pad_maximum_fusion.3), channel_id=1, source_target_pairs={{0,16},{1,17},{2,18},{3,19},{4,20},{5,21},{6,22},{7,23},{8,24},{9,... | collective-permute-start | bytes 7077896 | tf_op jit(solution)/shard_map/ppermute | solution.py:20
  1016.3 4.8 copy-start.1
  (22 other events, 64.4 us)
Sparse Core Ops, SparseCore 0:
  143.0 98.9 reduce-scatter.18
  247.7 95.2 reduce-scatter.20
  348.0 95.2 reduce-scatter.22
  448.3 95.2 reduce-scatter.24
  549.5 117.5 reduce-scatter.14
  673.9 106.0 reduce-scatter.16
